TPU v7x, 512 devices: a whole 4x8x8 slice. The times are simulated.
512 devices in a mesh: row: 16 (over z, core), col: 32 (over y, x).
Axes of the slice: x: 4, y: 8, z: 8, core: 2. Of those that a mesh axis runs over, the one named last changes fastest.
Arguments:
- points: float32 [16, 16384], P(None, ('row', 'col')), may hold values from -6 to 6
- pivots_first: int32 [128], replicated, may hold values from 0 to 16383, as said below
- pivots_second: int32 [128], replicated, may hold values from 0 to 16383, as said below
Outputs:
- panels: float32 [16384, 256], P('row')
- schur: float32 [16384, 16384], P('row', 'col')
Inputs may be any that keep to these rules, and one draw needn't show every extreme that they name: `pivots_first`: 128 distinct indices, none of them among pivots_second. `pivots_second`: 128 distinct indices, none of them among pivots_first.
All inputs are finite; a program needn't handle non-finite values.
Results may differ from a plain program's by a relative error of at most 0.0003.
Values sent between devices are 32-bit elements; how exact they have to be, the bound alone decides.
A program may use at most 64 MiB of HBM per device.

v0:
```python
import jax
import jax.numpy as jnp
from jax import lax
from jax.sharding import PartitionSpec as P

DIM = 16
BLOCK = 128


def laid_out(pieces, dim):
    lengths = list(pieces.shape[1:])
    lengths[dim] *= pieces.shape[0]
    return jnp.moveaxis(pieces, 0, dim).reshape(lengths)


def sent_to_all(x, axis):
    devices = lax.axis_size(axis)
    return lax.all_to_all(jnp.broadcast_to(x[None], (devices, *x.shape)), axis, 0, 0, tiled=True)


def gather_directly(x, axis, dim):
    return laid_out(sent_to_all(x, axis), dim)


def kernel(left, left_ids, right, right_ids):
    left_sq = jnp.sum(left * left, axis=0)
    right_sq = jnp.sum(right * right, axis=0)
    inner = jnp.dot(left.T, right, precision=lax.Precision.HIGHEST)
    dist = left_sq[:, None] + right_sq[None, :] - 2.0 * inner
    same = (left_ids[:, None] == right_ids[None, :]).astype(jnp.float32)
    return jnp.exp(-dist / DIM) + 0.1 * same


def right_solve(root, columns):
    return jax.scipy.linalg.solve_triangular(root, columns.T, lower=True).T


def per_device(points, pivots_first, pivots_second):
    per_dev = points.shape[1]
    n_row = lax.axis_size("row")
    n_col = lax.axis_size("col")
    row_idx = lax.axis_index("row")
    col_idx = lax.axis_index("col")
    rows_blk = per_dev * n_col
    cols_blk = per_dev * n_row
    row_pts = gather_directly(points, "col", 1)
    row_ids = row_idx * rows_blk + jnp.arange(rows_blk, dtype=jnp.int32)
    col_ids = col_idx * cols_blk + jnp.arange(cols_blk, dtype=jnp.int32)
    both_pivots = jnp.concatenate([pivots_first, pivots_second])
    everything = gather_directly(row_pts, "row", 1)
    col_pts = lax.dynamic_slice_in_dim(everything, col_idx * cols_blk, cols_blk, 1)
    pivot_pts = jnp.take(everything, both_pivots, axis=1)
    first_pts = pivot_pts[:, :BLOCK]
    second_pts = pivot_pts[:, BLOCK:]
    first_root = jnp.linalg.cholesky(kernel(first_pts, pivots_first, first_pts, pivots_first))
    first_rows = right_solve(first_root, kernel(row_pts, row_ids, first_pts, pivots_first))
    first_cols = right_solve(first_root, kernel(col_pts, col_ids, first_pts, pivots_first))
    first_pivot = right_solve(
        first_root, kernel(second_pts, pivots_second, first_pts, pivots_first)
    )
    pivot_block = kernel(second_pts, pivots_second, second_pts, pivots_second) - jnp.dot(
        first_pivot, first_pivot.T, precision=lax.Precision.HIGHEST
    )
    second_root = jnp.linalg.cholesky(pivot_block)
    second_rows = kernel(row_pts, row_ids, second_pts, pivots_second) - jnp.dot(
        first_rows, first_pivot.T, precision=lax.Precision.HIGHEST
    )
    second_rows = right_solve(second_root, second_rows)
    second_cols = kernel(col_pts, col_ids, second_pts, pivots_second) - jnp.dot(
        first_cols, first_pivot.T, precision=lax.Precision.HIGHEST
    )
    second_cols = right_solve(second_root, second_cols)
    panel_rows = jnp.concatenate([first_rows, second_rows], axis=1)
    panel_cols = jnp.concatenate([first_cols, second_cols], axis=1)
    schur = kernel(row_pts, row_ids, col_pts, col_ids) - jnp.dot(
        panel_rows, panel_cols.T, precision=lax.Precision.HIGHEST
    )
    return (panel_rows, schur)


def solution(mesh):
    return jax.shard_map(
        per_device,
        mesh=mesh,
        in_specs=(P(None, ("row", "col")), P(), P()),
        out_specs=(P("row", None), P("row", "col")),
        check_vma=False,
    )
```

profile of v0, /device:TPU:1, one launch (start us, length us, event | category | flops | bytes accessed | tf_op | source)
XLA Modules:
  0.0 141.1 jit_solution(16211600179101285530)
XLA Ops:
  0.6 0.7 broadcast_in_dim.17
  1.5 19.1 %all_to_all.10 = f32[32,1,512]{2,1,0:T(1,128)S(1)} all-to-all(f32[32,1,512]{2,1,0:T(1,128)S(1)} %reshape.152), channel_id=1, replica_groups=mesh['row'=16,'col'=32] {'col'}, dimensions={0} | all-to-all | bytes 131072 | tf_op jit(solution)/shard_map/all_to_all | solution.py:18
  20.6 0.5 broadcast.253
  21.1 0.8 reduce.5
  22.3 1.1 broadcast_in_dim.20
  23.4 12.4 %all-to-all-start.1 = ((f32[16,16,1024]{2,1,0:T(8,128)}), f32[16,16,1024]{2,1,0:T(8,128)S(1)}, u32[]{:S(2)}, u32[]{:S(2)}) async-start(f32[16,16,1024]{2,1,0:T(8,128)} %broadcast_in_dim.20), calls=%async_computation.1 | async-start | bytes 2097152 | tf_op jit(solution)/shard_map/all_to_all | solution.py:18
  36.1 27.7 %all-to-all-done.1 = f32[16,16,1024]{2,1,0:T(8,128)S(1)} async-done(((f32[16,16,1024]{2,1,0:T(8,128)}), f32[16,16,1024]{2,1,0:T(8,128)S(1)}, u32[]{:S(2)}, u32[]{:S(2)}) %all-to-all-start.1) | async-done | bytes 1048608 | tf_op jit(solution)/shard_map/all_to_all | solution.py:18
  63.8 4.6 %copy.22 = f32[16,16,1024]{0,2,1:T(8,128)} copy(f32[16,16,1024]{2,0,1:T(8,128)S(1)} %bitcast.78) | data formatting | bytes 2097152 | tf_op jit(solution)/shard_map/transpose | solution.py:13
  68.4 4.1 %gather_fusion = f32[256,16]{1,0:T(8,128)S(1)} fusion(f32[16,16384]{0,1:T(8,128)} %bitcast.71, s32[1024]{0:T(1024)S(1)} %pad_clamp_fusion), kind=kCustom, calls=%fused_computation | custom fusion | bytes 33792 | tf_op jit(solution)/shard_map/jit(_take)/gather | solution.py:52
  73.6 1.1 multiply_reduce_fusion
  74.7 1.4 fusion.23
  76.1 1.4 fusion.24
  77.5 4.0 %fusion.45 = f32[512,1024]{1,0:T(8,128)} fusion(f32[16,1024]{1,0:T(8,128)S(1)} %broadcast_in_dim.19, f32[16,16384]{0,1:T(8,128)} %bitcast.75, s32[]{:T(128)S(6)} %select_n.29), kind=kOutput, calls=%fused_computation.62 | convolution fusion | flops 100663296 | bytes 2424836 | tf_op jit(solution)/shard_map/dot_general | solution.py:28
  81.6 0.7 fusion.14
  82.2 0.7 fusion.9
  83.1 11.7 %cholesky.44 = f32[128,128]{1,0:T(8,128)S(1)} custom-call(f32[128,128]{1,0:T(8,128)S(1)} %copy.24), custom_call_target="Cholesky" | custom-call | tf_op jit(solution)/shard_map/jit(cholesky)/cholesky | solution.py:55
  94.9 0.6 compare_reduce_fusion.1
  95.5 0.7 fusion.47
  96.2 9.8 %custom-call.15 = f32[1,128,128]{1,2,0:T(8,128)S(1)} custom-call(f32[1,128,128]{2,1,0:T(8,128)S(1)} %fusion.47), custom_call_target="InvertDiagBlocksLowerTriangular" | custom-call | tf_op jit(solution)/shard_map/jit(_solve_triangular)/triangular_solve | solution.py:35
  106.8 11.9 %cholesky.55 = f32[128,128]{1,0:T(8,128)S(1)} custom-call(f32[128,128]{1,0:T(8,128)S(1)} %copy.26), custom_call_target="Cholesky" | custom-call | tf_op jit(solution)/shard_map/jit(cholesky)/cholesky | solution.py:64
  118.7 0.6 compare_reduce_fusion
  119.4 0.7 fusion.48
  120.0 9.8 %custom-call.16 = f32[1,128,128]{1,2,0:T(8,128)S(1)} custom-call(f32[1,128,128]{2,1,0:T(8,128)S(1)} %fusion.48), custom_call_target="InvertDiagBlocksLowerTriangular" | custom-call | tf_op jit(solution)/shard_map/jit(_solve_triangular)/triangular_solve | solution.py:35
  129.9 0.4 fusion.52
  130.3 0.6 fusion.56
  130.9 0.4 convolution_subtract_fusion.1
  131.4 1.1 convolution_bitcast_fusion.1
  132.5 0.6 convolution_subtract_fusion
  133.1 0.6 convolution_bitcast_fusion
  133.9 1.3 copy.28
  135.2 4.1 %fusion.4 = f32[1024,512]{0,1:T(8,128)S(1)} fusion(f32[512,1024]{1,0:T(8,128)} %fusion.45, s32[1024]{0:T(1024)S(1)} %iota_add_fusion, f32[512]{0:T(512)S(1)} %multiply_reduce_fusion, f32[1024]{0:T(1024)S(1)} %add.200, s32[512]{0:T(512)S(1)} %iota_add_fusion.1, f32[512,128]{0,1:T(8,128)} %convolution_bitcast_fusion.1, f32[512,128]{0,1:T(8,128)S(1)} %bitcast.80, ...), kind=kOutput, calls=%fused_computation.6 | convolution fusion | flops 1615724544 | bytes 5779456 | tf_op jit(solution)/shard_map/dot_general | solution.py:75
  139.3 1.8 %copy.29 = f32[1024,512]{1,0:T(8,128)} copy(f32[1024,512]{0,1:T(8,128)S(1)} %fusion.4) | data formatting | bytes 4194304
  (34 shorter events, 2.9 us)
Async XLA Ops:
  22.1 13.8 %copy-start.1 = (s32[128]{0:T(128)S(1)}, s32[128]{0:T(128)}, u32[]{:S(2)}) copy-start(s32[128]{0:T(128)} %param.9) | copy-start | bytes 1540
  22.1 13.8 %copy-start = (s32[128]{0:T(128)S(1)}, s32[128]{0:T(128)}, u32[]{:S(2)}) copy-start(s32[128]{0:T(128)} %param.10) | copy-start | bytes 1540
  23.4 40.4 %all-to-all-start.1 = ((f32[16,16,1024]{2,1,0:T(8,128)}), f32[16,16,1024]{2,1,0:T(8,128)S(1)}, u32[]{:S(2)}, u32[]{:S(2)}) async-start(f32[16,16,1024]{2,1,0:T(8,128)} %broadcast_in_dim.20), calls=%async_computation.1 | async-start | bytes 2097152 | tf_op jit(solution)/shard_map/all_to_all | solution.py:18
where the time goes:
time: 142 us; the launch traced here: 141 us
  other arithmetic  48.2 us (34%)
  waiting for transfers between devices  27.7 us (20%)
  blocking collectives  19.1 us (13%)
  matrix products  17.6 us (12%)
  local copies, waits for them, and re-layouts  15.1 us (11%)
  starting transfers between devices  12.4 us (9%)
    all_to_all x1, waiting for transfers between devices, sent_to_all(): lax.all_to_all(jnp.broadcast_to(x[None], (devices, *x.shape)), axis, 0, 0...  27.7 us
    another operation x4, other arithmetic, right_solve(): return jax.scipy.linalg.solve_triangular(root, columns.T, lower=True).T  20.9 us
    all_to_all x1, blocking collectives, sent_to_all(): lax.all_to_all(jnp.broadcast_to(x[None], (devices, *x.shape)), axis, 0, 0...  19.1 us
    another operation x3, other arithmetic, per_device(): second_root = jnp.linalg.cholesky(pivot_block)  12.6 us
    all_to_all x1, starting transfers between devices, sent_to_all(): lax.all_to_all(jnp.broadcast_to(x[None], (devices, *x.shape)), axis, 0, 0...  12.4 us
    another operation x3, other arithmetic, per_device(): jnp.linalg.cholesky(kernel(first_pts, pivots_first, first_pts, pivots_fir...  12.4 us
    dot_general x8, matrix products, kernel(): inner = jnp.dot(left.T, right, precision=lax.Precision.HIGHEST)  9.02 us
    transpose x2, local copies, waits for them, and re-layouts, laid_out(): return jnp.moveaxis(pieces, 0, dim).reshape(lengths)  4.7 us
  transfers between devices with their start and end apart: 1, of which 1 were waited for; matrix products, arithmetic and copies ran while one was open for 0% of the time, Pallas kernels for 0%

commit v1 on v0

v1 whole, which is shorter than its diff:
```python
import functools
import jax
import jax.numpy as jnp
from jax import lax
from jax.sharding import PartitionSpec as P
from jax.experimental import pallas as pl
from jax.experimental.pallas import tpu as pltpu

DIM = 16
BLOCK = 128
PIV = 2 * BLOCK
LEAF = 32
bf16 = jnp.bfloat16
f32 = jnp.float32


def split3(x):
    hi = x.astype(bf16)
    r = x - hi.astype(f32)
    mid = r.astype(bf16)
    lo = (r - mid.astype(f32)).astype(bf16)
    return hi, mid, lo


def dot(a, b):
    return lax.dot_general(a, b, (((1,), (0,)), ((), ())), preferred_element_type=f32)


def features(pts, left):
    n = pts.shape[1]
    sq = jnp.sum(pts * pts, axis=0, keepdims=True) * (-1.0 / DIM)
    sh, sm, sl = split3(sq)
    if not left:
        pts = pts * (2.0 / DIM)
    h, m, l = split3(pts)
    row = lax.broadcasted_iota(jnp.int32, (DIM, n), 0)
    at = 0 if left else 3
    ext = jnp.where((row >= 3 - at) & (row < 6 - at), 1.0, 0.0).astype(f32)
    for i, part in enumerate((sh, sm, sl)):
        ext = jnp.where(row == at + i, jnp.broadcast_to(part.astype(f32), (DIM, n)), ext)
    ext = ext.astype(bf16)
    zero = jnp.zeros((DIM, n), bf16)
    parts = (h, h, m, m, h, l, ext, zero) if left else (h, m, h, m, l, h, ext, zero)
    return jnp.concatenate(parts, axis=0)


def leaf(a_ref, o):
    rows = a_ref[pl.ds(o, LEAF), :]
    half = (o // 128) * 128
    tile = rows[:, half:half + 128]
    lane = lax.broadcasted_iota(jnp.int32, (LEAF, PIV), 1)
    sub = lax.broadcasted_iota(jnp.int32, (LEAF, PIV), 0)
    inside = (lane >= o) & (lane < o + LEAF)
    r = jnp.where(inside, jnp.where(lane == sub + o, 1.0, 0.0), rows)
    w = o - half
    v = [jnp.broadcast_to(tile[:, w + m:w + m + 1], (LEAF, 128)) for m in range(LEAF)]
    G = LEAF // 8
    v = [[x[8 * g:8 * g + 8] for g in range(G)] for x in v]
    r = [[r[8 * g:8 * g + 8, 128 * h:128 * h + 128] for h in range(PIV // 128)] for g in range(G)]
    sub8 = lax.broadcasted_iota(jnp.int32, (8, 128), 0)
    ds = []

    def row_of(x, i):
        return jnp.broadcast_to(x[i:i + 1, :], (8, 128))

    for c in range(LEAF):
        g0, i0 = c // 8, c % 8
        d = row_of(v[c][g0], i0)
        ds.append(d)
        inv = 1.0 / d
        mult = {}
        for g in range(g0, G):
            x = v[c][g]
            if g == g0:
                if i0 == 7:
                    continue
                x = jnp.where(sub8 > i0, x, 0.0)
            mult[g] = x * inv
        for m in range(c + 1, LEAF):
            p = row_of(v[m][g0], i0)
            for g in mult:
                v[m][g] = v[m][g] - mult[g] * p
        for h in range(PIV // 128):
            p = row_of(r[g0][h], i0)
            for g in mult:
                r[g][h] = r[g][h] - mult[g] * p
    out = []
    for g in range(G):
        d = ds[8 * g]
        for i in range(1, 8):
            d = jnp.where(sub8 == i, ds[8 * g + i], d)
        s = lax.rsqrt(d)
        out.append(jnp.concatenate([x * s for x in r[g]], axis=1))
    return jnp.concatenate(out, axis=0)


def factor(a_ref):
    for k in range(PIV // LEAF):
        o = k * LEAF
        u = leaf(a_ref, o)
        lane = lax.broadcasted_iota(jnp.int32, (LEAF, PIV), 1)
        a_ref[pl.ds(o, LEAF), :] = jnp.where(lane < o + LEAF, u, 0.0)
        left = PIV - o - LEAF
        if left:
            h, m, l = split3(u)
            lhs = jnp.concatenate((h, h, m, m, h, l), axis=0)
            rhs = jnp.concatenate((h, m, h, m, l, h), axis=0)
            start = ((o + LEAF) // 128) * 128
            lt = lhs[:, start:].T
            lt = lt[o + LEAF - start:, :]
            upd = dot(lt, rhs)
            lane = lax.broadcasted_iota(jnp.int32, (left, PIV), 1)
            old = a_ref[pl.ds(o + LEAF, left), :]
            old = jnp.where((lane >= o) & (lane < o + LEAF), 0.0, old)
            a_ref[pl.ds(o + LEAF, left), :] = old - upd


def dot6(ls, rs):
    lh, lm, ll = ls
    rh, rm, rl = rs
    return (dot(ll, rh) + dot(lh, rl) + dot(lm, rm)) + (dot(lm, rh) + dot(lh, rm)) + dot(lh, rh)


def dot3(ls, rs):
    lh, lm = ls[:2]
    rh, rm = rs[:2]
    return (dot(lm, rh) + dot(lh, rm)) + dot(lh, rh)


def kernel_b(base_ref, pivl_ref, pivs_ref, pt_ref, rt_ref, ct_ref, panel_ref, schur_ref,
             a_ref, fr_ref, fp_ref, fc_ref, wt_ref, pc_ref, *, tile, six):
    t = pl.program_id(0)
    n_rows, n_cols = rt_ref.shape[1], ct_ref.shape[1]

    @pl.when(t == 0)
    def _():
        pt = pt_ref[...]
        fp = features(pt, False)
        fp_ref[...] = fp
        fpl = features(pt, True).T
        kpp = jnp.exp(dot(fpl, fp))
        i = lax.broadcasted_iota(jnp.int32, (PIV, PIV), 0)
        j = lax.broadcasted_iota(jnp.int32, (PIV, PIV), 1)
        a_ref[...] = jnp.where(i == j, kpp + 0.1, kpp)
        fr_ref[...] = features(rt_ref[...], True).T
        fc = features(ct_ref[...], False)
        fc_ref[...] = fc
        factor(a_ref)
        w = a_ref[...]
        kpc = jnp.exp(dot(fpl, fc))
        cid = base_ref[1] + lax.broadcasted_iota(jnp.int32, (PIV, n_cols), 1)
        kpc = kpc + jnp.where(cid == pivs_ref[...], 0.1, 0.0)
        pc = dot6(split3(w), split3(kpc))
        for q, x in enumerate(split3(pc)):
            pc_ref[q] = x
        for q, x in enumerate(split3(w.T)):
            wt_ref[q] = x

    fr = fr_ref[pl.ds(pl.multiple_of(t * tile, tile), tile), :]
    krp = jnp.exp(dot(fr, fp_ref[...]))
    rid = base_ref[0] + t * tile + lax.broadcasted_iota(jnp.int32, (tile, PIV), 0)
    krp = krp + jnp.where(rid == pivl_ref[...], 0.1, 0.0)
    panel = dot6(split3(krp), (wt_ref[0], wt_ref[1], wt_ref[2]))
    panel_ref[...] = panel
    krc = jnp.exp(dot(fr, fc_ref[...]))
    off = base_ref[1] - base_ref[0] - t * tile
    i = lax.broadcasted_iota(jnp.int32, (tile, n_cols), 0)
    j = lax.broadcasted_iota(jnp.int32, (tile, n_cols), 1)
    krc = krc + jnp.where(i == j + off, 0.1, 0.0)
    mul = dot6 if six else dot3
    schur_ref[...] = krc - mul(split3(panel), (pc_ref[0], pc_ref[1], pc_ref[2]))


def compute(base, pivots, pt, rt, ct, tile=128, six=True):
    n_rows, n_cols = rt.shape[1], ct.shape[1]
    whole = lambda x: pl.BlockSpec(x.shape, lambda t: (0,) * x.ndim)
    pivl = pivots[None, :]
    pivs = pivots[:, None]
    return pl.pallas_call(
        functools.partial(kernel_b, tile=tile, six=six),
        grid=(n_rows // tile,),
        out_shape=(
            jax.ShapeDtypeStruct((n_rows, PIV), f32),
            jax.ShapeDtypeStruct((n_rows, n_cols), f32),
        ),
        in_specs=[pl.BlockSpec(memory_space=pltpu.SMEM)] + [whole(x) for x in (pivl, pivs, pt, rt, ct)],
        out_specs=(
            pl.BlockSpec((tile, PIV), lambda t: (t, 0)),
            pl.BlockSpec((tile, n_cols), lambda t: (t, 0)),
        ),
        scratch_shapes=[
            pltpu.VMEM((PIV, PIV), f32),
            pltpu.VMEM((n_rows, 128), bf16),
            pltpu.VMEM((128, PIV), bf16),
            pltpu.VMEM((128, n_cols), bf16),
            pltpu.VMEM((3, PIV, PIV), bf16),
            pltpu.VMEM((3, PIV, n_cols), bf16),
        ],
        compiler_params=pltpu.CompilerParams(vmem_limit_bytes=48 << 20),
    )(base, pivl, pivs, pt, rt, ct)


MESH = pl.DeviceIdType.MESH


def gather_kernel(nz, ny, nx, pts_ref, own_ref, piv_ref, piv_out, row_out, col_out,
                  contrib, rs_buf, y_src, y_buf, z_src, z_buf,
                  rs_send, rs_recv, y_send, y_recv, z_send, z_recv, ag_send, ag_recv,
                  row_send, row_recv, col_send, col_recv):
    n_row, n_col = 2 * nz, ny * nx
    row = lax.axis_index("row")
    col = lax.axis_index("col")
    core, z = row % 2, row // 2
    x, y = col % nx, col // nx
    ring = 2 * nx
    me = 2 * x + core

    def ring_dev(u):
        return (2 * z + u % 2, nx * y + u // 2)

    def y_dev(d):
        return (row, nx * ((y + d) % ny) + x)

    def z_dev(d):
        return (2 * ((z + d) % nz) + core, col)

    def row_dev(d):
        return (row, (col + d) % n_col)

    wide = n_col // n_row
    per = n_col // wide
    target = wide * row + col // per
    part = col % per
    source = col // wide
    first = (col % wide) * per

    barrier = pltpu.get_barrier_semaphore()

    def signal(dev):
        pl.semaphore_signal(barrier, inc=1, device_id=dev, device_id_type=MESH)

    def loop(lo, hi, f):
        def body(i, carry):
            f(i)
            return carry
        lax.fori_loop(lo, hi, body, 0)

    loop(1, ring, lambda d: signal(ring_dev((me + d) % ring)))
    loop(1, ny, lambda d: signal(y_dev(d)))
    loop(1, nz, lambda d: signal(z_dev(d)))
    loop(1, n_col, lambda d: signal(row_dev(d)))

    self_source = jnp.logical_and(source == row, col // per == col % wide)

    def greet_source(i):
        @pl.when(jnp.logical_or(source != row, first + i != col))
        def _():
            signal((source, first + i))

    loop(0, per, greet_source)

    pts = pts_ref[...]
    n = pts.shape[1]
    mine = (row * n_col + col) * n
    hit = piv_ref[...] == mine + lax.broadcasted_iota(jnp.int32, (n, PIV), 0)
    hot = jnp.where(hit, 1.0, 0.0).astype(bf16)
    h, m, l = split3(pts)
    got = (dot(l, hot) + dot(m, hot)) + dot(h, hot)
    quarter = 4
    for u in range(8):
        half, c4 = u // 4, u % 4
        contrib[u] = got[4 * c4:4 * c4 + 4, 128 * half:128 * half + 128]
    row_out[col] = own_ref[...]

    to_me = n_row - 1 + jnp.where(target == col, 0, 1)
    pl.semaphore_wait(barrier, (ring - 1) + (ny - 1) + (nz - 1) + (n_col - 1) + to_me)

    def rs_copy(d):
        u = (me + d) % ring
        return pltpu.make_async_remote_copy(
            src_ref=contrib.at[u], dst_ref=rs_buf.at[d - 1], send_sem=rs_send.at[d - 1],
            recv_sem=rs_recv.at[d - 1], device_id=ring_dev(u), device_id_type=MESH)

    def y_copy(d):
        return pltpu.make_async_remote_copy(
            src_ref=y_src, dst_ref=y_buf.at[d - 1], send_sem=y_send.at[d - 1],
            recv_sem=y_recv.at[d - 1], device_id=y_dev(d), device_id_type=MESH)

    def z_copy(d):
        return pltpu.make_async_remote_copy(
            src_ref=z_src, dst_ref=z_buf.at[d - 1], send_sem=z_send.at[d - 1],
            recv_sem=z_recv.at[d - 1], device_id=z_dev(d), device_id_type=MESH)

    def ag_copy(d):
        return pltpu.make_async_remote_copy(
            src_ref=piv_out.at[me], dst_ref=piv_out.at[me], send_sem=ag_send.at[d - 1],
            recv_sem=ag_recv.at[d - 1], device_id=ring_dev((me + d) % ring), device_id_type=MESH)

    def row_copy(d):
        return pltpu.make_async_remote_copy(
            src_ref=own_ref, dst_ref=row_out.at[col], send_sem=row_send.at[d - 1],
            recv_sem=row_recv.at[d - 1], device_id=row_dev(d), device_id_type=MESH)

    def col_copy(d):
        return pltpu.make_async_remote_copy(
            src_ref=own_ref, dst_ref=col_out.at[part], send_sem=col_send.at[d],
            recv_sem=col_recv.at[part], device_id=((row + d) % n_row, target), device_id_type=MESH)

    def col_arrival(i):
        return pltpu.make_async_remote_copy(
            src_ref=own_ref, dst_ref=col_out.at[i], send_sem=col_send.at[0],
            recv_sem=col_recv.at[i], device_id=(row, col), device_id_type=MESH)

    for d in range(1, ring):
        rs_copy(d).start()
    loop(1, n_col, lambda d: row_copy(d).start())

    @pl.when(target != col)
    def _():
        col_copy(0).start()

    @pl.when(target == col)
    def _():
        col_out[part] = own_ref[...]

    loop(1, n_row, lambda d: col_copy(d).start())

    total = contrib[me]
    for d in range(1, ring):
        rs_copy(d).wait_recv()
        total = total + rs_buf[d - 1]
    y_src[...] = total
    for d in range(1, ny):
        y_copy(d).start()
    for d in range(1, ny):
        y_copy(d).wait_recv()
        total = total + y_buf[d - 1]
    z_src[...] = total
    for d in range(1, nz):
        z_copy(d).start()
    for d in range(1, nz):
        z_copy(d).wait_recv()
        total = total + z_buf[d - 1]
    piv_out[me] = total
    for d in range(1, ring):
        ag_copy(d).start()
    loop(1, n_col, lambda d: row_copy(d).wait_recv())

    def take(i):
        @pl.when(jnp.logical_or(source != row, first + i != col))
        def _():
            col_arrival(i).wait_recv()

    loop(0, per, take)
    for d in range(1, ring):
        ag_copy(d).wait_recv()
    for d in range(1, ring):
        rs_copy(d).wait_send()
        ag_copy(d).wait_send()
    for d in range(1, ny):
        y_copy(d).wait_send()
    for d in range(1, nz):
        z_copy(d).wait_send()
    loop(1, n_col, lambda d: row_copy(d).wait_send())

    @pl.when(target != col)
    def _():
        col_copy(0).wait_send()

    loop(1, n_row, lambda d: col_copy(d).wait_send())


def gather(points, pivots, mesh):
    n_row, n_col = mesh.shape["row"], mesh.shape["col"]
    nz, nx = n_row // 2, 4
    ny = n_col // nx
    ring = 2 * nx
    own = points.reshape(4, 128)
    dma = pltpu.SemaphoreType.DMA
    vmem = pl.BlockSpec(memory_space=pltpu.VMEM)
    piv, rows, cols = pl.pallas_call(
        functools.partial(gather_kernel, nz, ny, nx),
        out_shape=(
            jax.ShapeDtypeStruct((ring, 4, 128), f32),
            jax.ShapeDtypeStruct((n_col, 4, 128), f32),
            jax.ShapeDtypeStruct((n_row, 4, 128), f32),
        ),
        in_specs=[vmem] * 3,
        out_specs=(vmem,) * 3,
        scratch_shapes=[
            pltpu.VMEM((ring, 4, 128), f32),
            pltpu.VMEM((ring - 1, 4, 128), f32),
            pltpu.VMEM((4, 128), f32),
            pltpu.VMEM((ny - 1, 4, 128), f32),
            pltpu.VMEM((4, 128), f32),
            pltpu.VMEM((nz - 1, 4, 128), f32),
            dma((ring - 1,)), dma((ring - 1,)),
            dma((ny - 1,)), dma((ny - 1,)),
            dma((nz - 1,)), dma((nz - 1,)),
            dma((ring - 1,)), dma((ring - 1,)),
            dma((n_col - 1,)), dma((n_col - 1,)),
            dma((n_row,)), dma((n_row,)),
        ],
        compiler_params=pltpu.CompilerParams(collective_id=0, has_side_effects=True),
    )(points, own, pivots[None, :])
    pt = piv.reshape(2, DIM, 128).transpose(1, 0, 2).reshape(DIM, PIV)

    def unpack(x):
        k = x.shape[0]
        return x.reshape(k, DIM, 32).transpose(1, 0, 2).reshape(DIM, k * 32)

    return pt, unpack(rows), unpack(cols)


def solution(mesh):
    def per_device(points, pivots_first, pivots_second):
        pivots = jnp.concatenate([pivots_first, pivots_second])
        pt, rt, ct = gather(points, pivots, mesh)
        base = jnp.stack([lax.axis_index("row") * rt.shape[1], lax.axis_index("col") * ct.shape[1]])
        return compute(base.astype(jnp.int32), pivots, pt, rt, ct)

    return jax.shard_map(
        per_device,
        mesh=mesh,
        in_specs=(P(None, ("row", "col")), P(), P()),
        out_specs=(P("row", None), P("row", "col")),
        check_vma=False,
    )
```

time: 142 us -> 61.2 us (0.43)
  Pallas kernels: 0 us -> 52.9 us
  other arithmetic: 48.2 us -> 0.08 us
  waiting for transfers between devices: 27.7 us -> 0 us
  blocking collectives: 19.1 us -> 0 us
  matrix products: 17.6 us -> 0 us
  starting transfers between devices: 12.4 us -> 0 us
  local copies, waits for them, and re-layouts: 15.1 us -> 7.1 us
    pallas_call x0 -> x2, Pallas kernels: none -> 52.9 us  [the longest x1 35.7 us: gather(): pl.pallas_call(functools.partial(gather_kernel, nz, ny, nx), out_shape=(j...]
    another operation x10 -> x1, other arithmetic: 45.9 us -> 0.08 us  [per_device(): jnp.stack([lax.axis_index('row') * rt.shape[1], lax.axis_index('col') * c...]
    all_to_all x1 -> x0, waiting for transfers between devices: 27.7 us -> none  [sent_to_all(): lax.all_to_all(jnp.broadcast_to(x[None], (devices, *x.shape)), axis, 0, 0...]
    all_to_all x1 -> x0, blocking collectives: 19.1 us -> none  [sent_to_all(): lax.all_to_all(jnp.broadcast_to(x[None], (devices, *x.shape)), axis, 0, 0...]
    dot_general x12 -> x0, matrix products: 14.5 us -> none  [the longest x8 9.02 us: kernel(): inner = jnp.dot(left.T, right, precision=lax.Precision.HIGHEST)]
    all_to_all x1 -> x0, starting transfers between devices: 12.4 us -> none  [sent_to_all(): lax.all_to_all(jnp.broadcast_to(x[None], (devices, *x.shape)), axis, 0, 0...]
    transpose x2 -> x0, local copies, waits for them, and re-layouts: 4.7 us -> none  [laid_out(): return jnp.moveaxis(pieces, 0, dim).reshape(lengths)]
    reshape x0 -> x8, local copies, waits for them, and re-layouts: none -> 4.28 us  [the longest x6 2.2 us: unpack(): return x.reshape(k, DIM, 32).transpose(1, 0, 2).reshape(DIM, k * 32)]
  transfers between devices with their start and end apart: 1 -> 0, of which waited for: 1 -> 0; matrix products, arithmetic and copies ran while one was open for 0% -> 0% of each run, Pallas kernels for 0% -> 0%
where the time goes in v1:
time: 61.2 us; the launch traced here: 60.8 us
  Pallas kernels  52.9 us (86%)
  local copies, waits for them, and re-layouts  7.1 us (12%)
  between operations  0.7 us (1%)
    pallas_call x1, Pallas kernels, gather(): pl.pallas_call(functools.partial(gather_kernel, nz, ny, nx), out_shape=(j...  35.7 us
    pallas_call x1, Pallas kernels, compute(): pl.pallas_call(functools.partial(kernel_b, tile=tile, six=six), grid=(n_r...  17.2 us
    reshape x6, local copies, waits for them, and re-layouts, unpack(): return x.reshape(k, DIM, 32).transpose(1, 0, 2).reshape(DIM, k * 32)  2.2 us
    reshape x1, local copies, waits for them, and re-layouts, gather(): own = points.reshape(4, 128)  1.35 us
    unnamed x6, local copies, waits for them, and re-layouts  1.34 us

profile of v1, /device:TPU:1, one launch (start us, length us, event | category | flops | bytes accessed | tf_op | source)
XLA Modules:
  0.0 60.8 jit_solution(6971394543516713411)
XLA Ops:
  0.6 0.1 pad_add_fusion.base_ref
  0.7 0.7 %constant_dynamic-update-slice_fusion.1 = s32[256]{0:T(256)S(1)} fusion(s32[256]{0:T(256)S(1)} %custom-call, s32[128]{0:T(128)} %param.4), kind=kLoop, calls=%fused_computation.4 | loop fusion | bytes 1024
  1.4 0.7 %constant_dynamic-update-slice_fusion = s32[256]{0:T(256)S(1)} fusion(s32[256]{0:T(256)S(1)} %constant_dynamic-update-slice_fusion.1, s32[128]{0:T(128)} %param.5), kind=kLoop, calls=%fused_computation.3 | loop fusion | bytes 1024 | tf_op jit(solution)/shard_map/concatenate | solution.py:417
  2.0 0.0 copy-start
  2.0 1.4 %reshape.25.own_ref = f32[4,128]{1,0:T(4,128)} reshape(f32[16,32]{1,0:T(8,128)} %pts_ref.1) | data formatting | bytes 4096 | tf_op jit(solution)/shard_map/reshape | solution.py:378
  3.4 0.0 copy-done
  3.4 35.7 %shard_map.50 = (f32[8,4,128]{2,1,0:T(4,128)}, f32[32,4,128]{2,1,0:T(4,128)}, f32[16,4,128]{2,1,0:T(4,128)}) custom-call(f32[16,32]{1,0:T(8,128)} %pts_ref.1, f32[4,128]{1,0:T(4,128)} %reshape.25.own_ref, s32[1,256]{1,0:T(1,128)} %bitcast.17), custom_call_target="tpu_custom_call" | custom-call | tf_op jit(solution)/shard_map/pallas_call | solution.py:381
  39.1 0.7 %copy.8 = f32[2,16,128]{2,0,1:T(2,128)S(1)} copy(f32[2,16,128]{2,1,0:T(8,128)} %bitcast.23) | data formatting | bytes 32768 | tf_op jit(solution)/shard_map/reshape | solution.py:406
  39.8 0.9 %reshape.30 = f32[16,16,32]{2,1,0:T(8,128)S(1)} reshape(f32[16,4,128]{2,1,0:T(4,128)} %get-tuple-element.7) | data formatting | bytes 65536 | tf_op jit(solution)/shard_map/reshape | solution.py:410
  40.7 0.1 reshape.31.ct_ref
  40.9 0.8 %copy.11.pivs_ref = s32[256,1]{1,0:T(8,128)S(1)} copy(s32[256,1]{0,1:T(1,128)} %bitcast.18) | data formatting | bytes 2048 | tf_op jit(solution)/shard_map/broadcast_in_dim | solution.py:178
  41.7 1.0 %reshape.28 = f32[32,16,32]{2,1,0:T(8,128)S(1)} reshape(f32[32,4,128]{2,1,0:T(4,128)} %get-tuple-element.6) | data formatting | bytes 131072 | tf_op jit(solution)/shard_map/reshape | solution.py:410
  42.6 0.1 copy.16
  42.7 0.1 reshape.29.rt_ref
  42.9 0.0 copy-start.1
  42.9 0.7 %copy-done.1 = s32[256]{0:T(256)S(1)} copy-done((s32[256]{0:T(256)S(1)}, s32[256]{0:T(256)}, u32[]{:S(2)}) %copy-start.1) | copy-done | bytes 1048
  43.6 17.2 %shard_map.51 = (f32[1024,256]{1,0:T(8,128)}, f32[1024,512]{1,0:T(8,128)}) custom-call(s32[2]{0:T(128)S(1)} %pad_add_fusion.base_ref, s32[1,256]{1,0:T(1,128)S(1)} %bitcast.19, s32[256,1]{1,0:T(8,128)S(1)} %copy.11.pivs_ref, f32[16,256]{1,0:T(8,128)S(1)} %bitcast.16, f32[16,1024]{1,0:T(8,128)S(1)} %reshape.29.rt_ref, f32[16,512]{1,0:T(8,128)S(1)} %reshape.31.ct_ref), custom_call_target="tpu_custom_call" | custom-call | tf_op jit(solution)/shard_map/pallas_call | solution.py:179
  (3 shorter events, 0.0 us)
Async XLA Ops:
  2.0 1.4 %copy-start = (s32[256]{0:T(256)}, s32[256]{0:T(256)S(1)}, u32[]{:S(2)}) copy-start(s32[256]{0:T(256)S(1)} %constant_dynamic-update-slice_fusion) | copy-start | bytes 3076
  42.9 0.7 %copy-start.1 = (s32[256]{0:T(256)S(1)}, s32[256]{0:T(256)}, u32[]{:S(2)}) copy-start(s32[256]{0:T(256)} %copy-done) | copy-start | bytes 3076

commit v2 on v1

v2 whole, which is shorter than its diff:
```python
import functools
import jax
import jax.numpy as jnp
from jax import lax
from jax.sharding import PartitionSpec as P
from jax.experimental import pallas as pl
from jax.experimental.pallas import tpu as pltpu

DIM = 16
BLOCK = 128
PIV = 2 * BLOCK
LEAF = 32
bf16 = jnp.bfloat16
f32 = jnp.float32


def split3(x):
    hi = x.astype(bf16)
    r = x - hi.astype(f32)
    mid = r.astype(bf16)
    lo = (r - mid.astype(f32)).astype(bf16)
    return hi, mid, lo


def dot(a, b):
    return lax.dot_general(a, b, (((1,), (0,)), ((), ())), preferred_element_type=f32)


def features(pts, left):
    n = pts.shape[1]
    sq = jnp.sum(pts * pts, axis=0, keepdims=True) * (-1.0 / DIM)
    sh, sm, sl = split3(sq)
    if not left:
        pts = pts * (2.0 / DIM)
    h, m, l = split3(pts)
    row = lax.broadcasted_iota(jnp.int32, (DIM, n), 0)
    at = 0 if left else 3
    ext = jnp.where((row >= 3 - at) & (row < 6 - at), 1.0, 0.0).astype(f32)
    for i, part in enumerate((sh, sm, sl)):
        ext = jnp.where(row == at + i, jnp.broadcast_to(part.astype(f32), (DIM, n)), ext)
    ext = ext.astype(bf16)
    zero = jnp.zeros((DIM, n), bf16)
    parts = (h, h, m, m, h, l, ext, zero) if left else (h, m, h, m, l, h, ext, zero)
    return jnp.concatenate(parts, axis=0)


def leaf(a_ref, o):
    rows = a_ref[pl.ds(o, LEAF), :]
    half = (o // 128) * 128
    tile = rows[:, half:half + 128]
    lane = lax.broadcasted_iota(jnp.int32, (LEAF, PIV), 1)
    sub = lax.broadcasted_iota(jnp.int32, (LEAF, PIV), 0)
    inside = (lane >= o) & (lane < o + LEAF)
    r = jnp.where(inside, jnp.where(lane == sub + o, 1.0, 0.0), rows)
    w = o - half
    v = [jnp.broadcast_to(tile[:, w + m:w + m + 1], (LEAF, 128)) for m in range(LEAF)]
    G = LEAF // 8
    v = [[x[8 * g:8 * g + 8] for g in range(G)] for x in v]
    r = [[r[8 * g:8 * g + 8, 128 * h:128 * h + 128] for h in range(PIV // 128)] for g in range(G)]
    sub8 = lax.broadcasted_iota(jnp.int32, (8, 128), 0)
    ds = []

    def row_of(x, i):
        return jnp.broadcast_to(x[i:i + 1, :], (8, 128))

    for c in range(LEAF):
        g0, i0 = c // 8, c % 8
        d = row_of(v[c][g0], i0)
        ds.append(d)
        inv = 1.0 / d
        mult = {}
        for g in range(g0, G):
            x = v[c][g]
            if g == g0:
                if i0 == 7:
                    continue
                x = jnp.where(sub8 > i0, x, 0.0)
            mult[g] = x * inv
        for m in range(c + 1, LEAF):
            p = row_of(v[m][g0], i0)
            for g in mult:
                v[m][g] = v[m][g] - mult[g] * p
        for h in range(PIV // 128):
            p = row_of(r[g0][h], i0)
            for g in mult:
                r[g][h] = r[g][h] - mult[g] * p
    out = []
    for g in range(G):
        d = ds[8 * g]
        for i in range(1, 8):
            d = jnp.where(sub8 == i, ds[8 * g + i], d)
        s = lax.rsqrt(d)
        out.append(jnp.concatenate([x * s for x in r[g]], axis=1))
    return jnp.concatenate(out, axis=0)


def factor(a_ref):
    for k in range(PIV // LEAF):
        o = k * LEAF
        u = leaf(a_ref, o)
        lane = lax.broadcasted_iota(jnp.int32, (LEAF, PIV), 1)
        a_ref[pl.ds(o, LEAF), :] = jnp.where(lane < o + LEAF, u, 0.0)
        left = PIV - o - LEAF
        if left:
            h, m, l = split3(u)
            lhs = jnp.concatenate((h, h, m, m, h, l), axis=0)
            rhs = jnp.concatenate((h, m, h, m, l, h), axis=0)
            start = ((o + LEAF) // 128) * 128
            lt = lhs[:, start:].T
            lt = lt[o + LEAF - start:, :]
            upd = dot(lt, rhs)
            lane = lax.broadcasted_iota(jnp.int32, (left, PIV), 1)
            old = a_ref[pl.ds(o + LEAF, left), :]
            old = jnp.where((lane >= o) & (lane < o + LEAF), 0.0, old)
            a_ref[pl.ds(o + LEAF, left), :] = old - upd


def dot6(ls, rs):
    lh, lm, ll = ls
    rh, rm, rl = rs
    return (dot(ll, rh) + dot(lh, rl) + dot(lm, rm)) + (dot(lm, rh) + dot(lh, rm)) + dot(lh, rh)


def dot3(ls, rs):
    lh, lm = ls[:2]
    rh, rm = rs[:2]
    return (dot(lm, rh) + dot(lh, rm)) + dot(lh, rh)


def kernel_b(pid_ref, pt_ref, fr_ref, fc_ref, panel_ref, schur_ref,
             a_ref, fp_ref, wt_ref, pc_ref, *, tile):
    t = pl.program_id(0)
    n_cols = fc_ref.shape[1]
    row0 = lax.axis_index("row") * fr_ref.shape[0] + t * tile
    col0 = lax.axis_index("col") * n_cols
    piv = pid_ref[...]

    @pl.when(t == 0)
    def _():
        pt = jnp.concatenate([pt_ref[0], pt_ref[1]], axis=1)
        fp = features(pt, False)
        fp_ref[...] = fp
        fpl = features(pt, True).T
        kpp = jnp.exp(dot(fpl, fp))
        i = lax.broadcasted_iota(jnp.int32, (PIV, PIV), 0)
        j = lax.broadcasted_iota(jnp.int32, (PIV, PIV), 1)
        a_ref[...] = jnp.where(i == j, kpp + 0.1, kpp)
        kpc = jnp.exp(dot(fpl, fc_ref[...]))
        ids = jnp.broadcast_to(piv.astype(f32), (8, PIV)).T[:, 0:1].astype(jnp.int32)
        cid = col0 + lax.broadcasted_iota(jnp.int32, (PIV, n_cols), 1)
        kpc = kpc + jnp.where(cid == ids, 0.1, 0.0)
        factor(a_ref)
        w = a_ref[...]
        pc = dot6(split3(w), split3(kpc))
        for q, x in enumerate(split3(pc)):
            pc_ref[q] = x
        for q, x in enumerate(split3(w.T)):
            wt_ref[q] = x

    fr = fr_ref[pl.ds(pl.multiple_of(t * tile, tile), tile), :]
    krp = jnp.exp(dot(fr, fp_ref[...]))
    rid = row0 + lax.broadcasted_iota(jnp.int32, (tile, PIV), 0)
    krp = krp + jnp.where(rid == piv, 0.1, 0.0)
    panel = dot6(split3(krp), (wt_ref[0], wt_ref[1], wt_ref[2]))
    panel_ref[...] = panel
    krc = jnp.exp(dot(fr, fc_ref[...]))
    i = lax.broadcasted_iota(jnp.int32, (tile, n_cols), 0)
    j = lax.broadcasted_iota(jnp.int32, (tile, n_cols), 1)
    krc = krc + jnp.where(i - j == col0 - row0, 0.1, 0.0)
    schur_ref[...] = krc - dot6(split3(panel), (pc_ref[0], pc_ref[1], pc_ref[2]))


def compute(pid, pt, fr, fc, tile=256):
    n_rows, n_cols = fr.shape[0], fc.shape[1]
    vmem = pl.BlockSpec(memory_space=pltpu.VMEM)
    return pl.pallas_call(
        functools.partial(kernel_b, tile=tile),
        grid=(n_rows // tile,),
        out_shape=(
            jax.ShapeDtypeStruct((n_rows, PIV), f32),
            jax.ShapeDtypeStruct((n_rows, n_cols), f32),
        ),
        in_specs=[vmem] * 4,
        out_specs=(
            pl.BlockSpec((tile, PIV), lambda t: (t, 0)),
            pl.BlockSpec((tile, n_cols), lambda t: (t, 0)),
        ),
        scratch_shapes=[
            pltpu.VMEM((PIV, PIV), f32),
            pltpu.VMEM((128, PIV), bf16),
            pltpu.VMEM((3, PIV, PIV), bf16),
            pltpu.VMEM((3, PIV, n_cols), bf16),
        ],
        compiler_params=pltpu.CompilerParams(vmem_limit_bytes=32 << 20),
    )(pid, pt, fr, fc)


MESH = pl.DeviceIdType.MESH
NX = 4


def loop(lo, hi, f):
    def body(i, carry):
        f(i)
        return carry
    lax.fori_loop(lo, hi, body, 0)


def unpack(buf_ref, out_ref):
    k = buf_ref.shape[0]
    tiles = k // 4
    lane = lax.broadcasted_iota(jnp.int32, (4 * tiles, 128), 1) // 32
    quads = []
    for q in range(4):
        quads.append(jnp.concatenate([buf_ref[4 * t + q] for t in range(tiles)], axis=0))
    for g in range(4):
        acc = quads[g]
        for q in range(4):
            if q != g:
                acc = jnp.where(lane == q, pltpu.roll(quads[q], (32 * (q - g)) % 128, 1), acc)
        for t in range(tiles):
            out_ref[4 * g:4 * g + 4, 128 * t:128 * t + 128] = acc[4 * t:4 * t + 4]


def gather_kernel(nz, ny, pts_hbm, pf_hbm, ps_hbm, pid_out, piv_out, fr_out, fc_out,
                  pts_ref, in_sem, own, contrib, c_buf, x_src, x_buf, y_src, y_buf, z_src, z_buf,
                  row_buf, col_buf, rt_ref, ct_ref,
                  c_send, c_recv, x_send, x_recv, y_send, y_recv, z_send, z_recv, ag_send, ag_recv,
                  row_send, row_recv, col_send, col_recv):
    n_row, n_col = 2 * nz, ny * NX
    row = lax.axis_index("row")
    col = lax.axis_index("col")
    core, z = row % 2, row // 2
    x, y = col % NX, col // NX
    other = (2 * z + 1 - core, col)

    def x_dev(d):
        return (row, NX * y + (x + d) % NX)

    def y_dev(d):
        return (row, NX * ((y + d) % ny) + x)

    def z_dev(d):
        return (2 * ((z + d) % nz) + core, col)

    def row_dev(d):
        return (row, (col + d) % n_col)

    wide = n_col // n_row
    per = n_col // wide
    target = wide * row + col // per
    part = col % per
    source = col // wide
    first = (col % wide) * per

    arrivals = [
        pltpu.make_async_copy(pts_hbm, pts_ref, in_sem.at[0]),
        pltpu.make_async_copy(pf_hbm, pid_out.at[:, pl.ds(0, BLOCK)], in_sem.at[1]),
        pltpu.make_async_copy(ps_hbm, pid_out.at[:, pl.ds(BLOCK, BLOCK)], in_sem.at[2]),
    ]
    for a in arrivals:
        a.start()
    barrier = pltpu.get_barrier_semaphore()

    def signal(dev):
        pl.semaphore_signal(barrier, inc=1, device_id=dev, device_id_type=MESH)

    signal(other)
    loop(1, nz, lambda d: signal(z_dev(d)))
    loop(1, n_col, lambda d: signal(row_dev(d)))

    def greet_source(i):
        @pl.when(jnp.logical_or(source != row, first + i != col))
        def _():
            signal((source, first + i))

    loop(0, per, greet_source)

    for a in arrivals:
        a.wait()
    pts = pts_ref[...]
    n = pts.shape[1]
    for g in range(4):
        own[:, 32 * g:32 * g + 32] = pts[4 * g:4 * g + 4, :]
    mine = (row * n_col + col) * n
    h, m, l = split3(pts)
    for half in range(2):
        hit = pid_out[:, BLOCK * half:BLOCK * half + BLOCK] == mine + lax.broadcasted_iota(jnp.int32, (n, BLOCK), 0)
        hot = jnp.where(hit, 1.0, 0.0).astype(bf16)
        contrib[half] = (dot(l, hot) + dot(m, hot)) + dot(h, hot)
    row_buf[col] = own[...]

    to_me = n_row - 1 + jnp.where(target == col, 0, 1)
    pl.semaphore_wait(barrier, 1 + (nz - 1) + (n_col - 1) + to_me)

    def remote(src, dst, send, recv, dev):
        return pltpu.make_async_remote_copy(
            src_ref=src, dst_ref=dst, send_sem=send, recv_sem=recv, device_id=dev, device_id_type=MESH)

    def c_copy():
        return remote(contrib.at[1 - core], c_buf, c_send, c_recv, other)

    def x_copy(d):
        return remote(x_src, x_buf.at[d - 1], x_send.at[d - 1], x_recv.at[d - 1], x_dev(d))

    def y_copy(d):
        return remote(y_src, y_buf.at[d - 1], y_send.at[d - 1], y_recv.at[d - 1], y_dev(d))

    def z_copy(d):
        return remote(z_src, z_buf.at[d - 1], z_send.at[d - 1], z_recv.at[d - 1], z_dev(d))

    def ag_copy():
        return remote(piv_out.at[core], piv_out.at[core], ag_send, ag_recv, other)

    def row_copy(d):
        return remote(own, row_buf.at[col], row_send.at[d - 1], row_recv.at[d - 1], row_dev(d))

    def col_copy(d):
        return remote(own, col_buf.at[part], col_send.at[d], col_recv.at[part], ((row + d) % n_row, target))

    def col_arrival(i):
        return remote(own, col_buf.at[i], col_send.at[0], col_recv.at[i], (row, col))

    c_copy().start()
    loop(1, n_col, lambda d: row_copy(d).start())

    @pl.when(target != col)
    def _():
        col_copy(0).start()

    @pl.when(target == col)
    def _():
        col_buf[part] = own[...]

    loop(1, n_row, lambda d: col_copy(d).start())

    c_copy().wait_recv()
    total = contrib[core] + c_buf[...]
    x_src[...] = total
    for d in range(1, NX):
        x_copy(d).start()
    for d in range(1, NX):
        x_copy(d).wait_recv()
        total = total + x_buf[d - 1]
    y_src[...] = total
    for d in range(1, ny):
        y_copy(d).start()
    for d in range(1, ny):
        y_copy(d).wait_recv()
        total = total + y_buf[d - 1]
    z_src[...] = total
    for d in range(1, nz):
        z_copy(d).start()

    loop(1, n_col, lambda d: row_copy(d).wait_recv())

    def take(i):
        @pl.when(jnp.logical_or(source != row, first + i != col))
        def _():
            col_arrival(i).wait_recv()

    loop(0, per, take)
    unpack(row_buf, rt_ref)
    unpack(col_buf, ct_ref)
    fr_out[...] = features(rt_ref[...], True).T
    fc_out[...] = features(ct_ref[...], False)

    for d in range(1, nz):
        z_copy(d).wait_recv()
        total = total + z_buf[d - 1]
    piv_out[core] = total
    ag_copy().start()
    c_copy().wait_send()
    for d in range(1, NX):
        x_copy(d).wait_send()
    for d in range(1, ny):
        y_copy(d).wait_send()
    for d in range(1, nz):
        z_copy(d).wait_send()
    loop(1, n_col, lambda d: row_copy(d).wait_send())

    @pl.when(target != col)
    def _():
        col_copy(0).wait_send()

    loop(1, n_row, lambda d: col_copy(d).wait_send())
    ag_copy().wait_recv()
    ag_copy().wait_send()


def gather(points, pf, ps, mesh):
    n_row, n_col = mesh.shape["row"], mesh.shape["col"]
    nz = n_row // 2
    ny = n_col // NX
    n = points.shape[1]
    dma = pltpu.SemaphoreType.DMA
    vmem = pl.BlockSpec(memory_space=pltpu.VMEM)
    return pl.pallas_call(
        functools.partial(gather_kernel, nz, ny),
        out_shape=(
            pltpu.VMEM((1, PIV), jnp.int32),
            pltpu.VMEM((2, DIM, BLOCK), f32),
            pltpu.VMEM((n * n_col, 128), bf16),
            pltpu.VMEM((128, n * n_row), bf16),
        ),
        in_specs=[pl.BlockSpec(memory_space=pltpu.HBM)] * 3,
        out_specs=(vmem,) * 4,
        scratch_shapes=[
            pltpu.VMEM((DIM, n), f32),
            dma((3,)),
            pltpu.VMEM((4, 128), f32),
            pltpu.VMEM((2, DIM, BLOCK), f32),
            pltpu.VMEM((DIM, BLOCK), f32),
            pltpu.VMEM((DIM, BLOCK), f32),
            pltpu.VMEM((NX - 1, DIM, BLOCK), f32),
            pltpu.VMEM((DIM, BLOCK), f32),
            pltpu.VMEM((ny - 1, DIM, BLOCK), f32),
            pltpu.VMEM((DIM, BLOCK), f32),
            pltpu.VMEM((nz - 1, DIM, BLOCK), f32),
            pltpu.VMEM((n_col, 4, 128), f32),
            pltpu.VMEM((n_row, 4, 128), f32),
            pltpu.VMEM((DIM, n * n_col), f32),
            pltpu.VMEM((DIM, n * n_row), f32),
            dma, dma,
            dma((NX - 1,)), dma((NX - 1,)),
            dma((ny - 1,)), dma((ny - 1,)),
            dma((nz - 1,)), dma((nz - 1,)),
            dma, dma,
            dma((n_col - 1,)), dma((n_col - 1,)),
            dma((n_row,)), dma((n_row,)),
        ],
        compiler_params=pltpu.CompilerParams(
            collective_id=0, has_side_effects=True, vmem_limit_bytes=8 << 20),
    )(points, pf, ps)


def solution(mesh):
    def per_device(points, pivots_first, pivots_second):
        points, pf, ps = (
            pltpu.with_memory_space_constraint(x, pltpu.HBM)
            for x in (points, pivots_first[None, :], pivots_second[None, :]))
        return compute(*gather(points, pf, ps, mesh))

    return jax.shard_map(
        per_device,
        mesh=mesh,
        in_specs=(P(None, ("row", "col")), P(), P()),
        out_specs=(P("row", None), P("row", "col")),
        check_vma=False,
    )
```

time: 61.2 us -> 49.2 us (0.80)
  local copies, waits for them, and re-layouts: 7.1 us -> 0 us
  Pallas kernels: 52.9 us -> 48.4 us
    pallas_call x2, Pallas kernels: 52.9 us -> 48.4 us  [the longest x1 33.3 us: gather(): pl.pallas_call(functools.partial(gather_kernel, nz, ny), out_shape=(pltpu...]
    reshape x8 -> x0, local copies, waits for them, and re-layouts: 4.28 us -> none  [the longest x6 2.2 us: unpack(): return x.reshape(k, DIM, 32).transpose(1, 0, 2).reshape(DIM, k * 32)]
    unnamed x6 -> x0, local copies, waits for them, and re-layouts: 1.34 us -> none
    broadcast_in_dim x1 -> x0, local copies, waits for them, and re-layouts: 0.81 us -> none  [compute(): pivs = pivots[:, None]]
    concatenate x1 -> x0, local copies, waits for them, and re-layouts: 0.67 us -> none  [per_device(): pivots = jnp.concatenate([pivots_first, pivots_second])]
where the time goes in v2:
time: 49.2 us; the launch traced here: 49.1 us
  Pallas kernels  48.4 us (98%)
  between operations  0.64 us (1%)
    pallas_call x1, Pallas kernels, gather(): pl.pallas_call(functools.partial(gather_kernel, nz, ny), out_shape=(pltpu...  33.3 us
    pallas_call x1, Pallas kernels, compute(): pl.pallas_call(functools.partial(kernel_b, tile=tile), grid=(n_rows // ti...  15.2 us

profile of v2, /device:TPU:1, one launch (start us, length us, event | category | flops | bytes accessed | tf_op | source)
XLA Modules:
  0.0 49.1 jit_solution(13662966770372982078)
XLA Ops:
  0.6 33.3 %shard_map.50 = (s32[1,256]{1,0:T(1,128)S(1)}, f32[2,16,128]{2,1,0:T(8,128)S(1)}, bf16[1024,128]{1,0:T(8,128)(2,1)S(1)}, bf16[128,512]{1,0:T(8,128)(2,1)S(1)}) custom-call(f32[16,32]{1,0:T(8,128)} %pts_hbm.1, s32[1,128]{1,0:T(1,128)} %bitcast.2, s32[1,128]{1,0:T(1,128)} %bitcast.3), custom_call_target="tpu_custom_call" | custom-call | tf_op jit(solution)/shard_map/pallas_call | solution.py:398
  33.9 15.2 %shard_map.51 = (f32[1024,256]{1,0:T(8,128)}, f32[1024,512]{1,0:T(8,128)}) custom-call(s32[1,256]{1,0:T(1,128)S(1)} %get-tuple-element.6.pid_ref, f32[2,16,128]{2,1,0:T(8,128)S(1)} %get-tuple-element.7.pt_ref, bf16[1024,128]{1,0:T(8,128)(2,1)S(1)} %get-tuple-element.8.fr_ref, bf16[128,512]{1,0:T(8,128)(2,1)S(1)} %get-tuple-element.9.fc_ref), custom_call_target="tpu_custom_call" | custom-call | tf_op jit(solution)/shard_map/pallas_call | solution.py:176

commit v3 on v2

--- a/solution.py
+++ b/solution.py
@@ -10,6 +10,7 @@
 BLOCK = 128
 PIV = 2 * BLOCK
 LEAF = 32
+SUB = 16
 bf16 = jnp.bfloat16
 f32 = jnp.float32
 
@@ -45,52 +46,61 @@
 
 
 def leaf(a_ref, o):
+    G, H = LEAF // 8, PIV // 128
     rows = a_ref[pl.ds(o, LEAF), :]
-    half = (o // 128) * 128
-    tile = rows[:, half:half + 128]
-    lane = lax.broadcasted_iota(jnp.int32, (LEAF, PIV), 1)
-    sub = lax.broadcasted_iota(jnp.int32, (LEAF, PIV), 0)
-    inside = (lane >= o) & (lane < o + LEAF)
-    r = jnp.where(inside, jnp.where(lane == sub + o, 1.0, 0.0), rows)
-    w = o - half
-    v = [jnp.broadcast_to(tile[:, w + m:w + m + 1], (LEAF, 128)) for m in range(LEAF)]
-    G = LEAF // 8
-    v = [[x[8 * g:8 * g + 8] for g in range(G)] for x in v]
-    r = [[r[8 * g:8 * g + 8, 128 * h:128 * h + 128] for h in range(PIV // 128)] for g in range(G)]
-    sub8 = lax.broadcasted_iota(jnp.int32, (8, 128), 0)
-    ds = []
+    r = [[rows[8 * g:8 * g + 8, 128 * h:128 * h + 128] for h in range(H)] for g in range(G)]
+    sub = lax.broadcasted_iota(jnp.int32, (8, 128), 0)
+    lane = lax.broadcasted_iota(jnp.int32, (8, 128), 1)
+    diag = [None] * LEAF
 
     def row_of(x, i):
         return jnp.broadcast_to(x[i:i + 1, :], (8, 128))
 
-    for c in range(LEAF):
-        g0, i0 = c // 8, c % 8
-        d = row_of(v[c][g0], i0)
-        ds.append(d)
-        inv = 1.0 / d
-        mult = {}
-        for g in range(g0, G):
-            x = v[c][g]
-            if g == g0:
-                if i0 == 7:
-                    continue
-                x = jnp.where(sub8 > i0, x, 0.0)
-            mult[g] = x * inv
-        for m in range(c + 1, LEAF):
-            p = row_of(v[m][g0], i0)
-            for g in mult:
-                v[m][g] = v[m][g] - mult[g] * p
-        for h in range(PIV // 128):
-            p = row_of(r[g0][h], i0)
-            for g in mult:
-                r[g][h] = r[g][h] - mult[g] * p
+    for s in range(0, LEAF, SUB):
+        h0, w = (o + s) // 128, (o + s) % 128
+        v = [[None if g < s // 8 else jnp.broadcast_to(r[g][h0][:, w + m:w + m + 1], (8, 128))
+              for g in range(G)] for m in range(SUB)]
+        inside = (lane >= w) & (lane < w + SUB)
+        for g in range(s // 8, G):
+            unit = jnp.where(lane == sub + w + 8 * g - s, 1.0, 0.0)
+            r[g][h0] = jnp.where(inside, unit, r[g][h0])
+        for c in range(0, SUB, 2):
+            g0, i0 = (s + c) // 8, (s + c) % 8
+            a, b, e = row_of(v[c][g0], i0), row_of(v[c + 1][g0], i0), row_of(v[c + 1][g0], i0 + 1)
+            det = a * e - b * b
+            inv = 1.0 / det
+            m1, m2 = {}, {}
+            for g in range(g0, G):
+                p, q = v[c][g], v[c + 1][g]
+                if g == g0:
+                    if i0 == 6:
+                        continue
+                    p, q = jnp.where(sub > i0 + 1, p, 0.0), jnp.where(sub > i0 + 1, q, 0.0)
+                m1[g] = (p * e - q * b) * inv
+                m2[g] = (q * a - p * b) * inv
+            for m in range(c + 2, SUB):
+                p, q = row_of(v[m][g0], i0), row_of(v[m][g0], i0 + 1)
+                for g in m1:
+                    v[m][g] = (v[m][g] - m1[g] * p) - m2[g] * q
+            ia = 1.0 / a
+            second = jnp.where(sub == i0 + 1, b * ia, 0.0)
+            for h in range(H):
+                p, q = row_of(r[g0][h], i0), row_of(r[g0][h], i0 + 1)
+                for g in m1:
+                    r[g][h] = (r[g][h] - m1[g] * p) - m2[g] * q
+                r[g0][h] = r[g0][h] - second * p
+            diag[s + c], diag[s + c + 1] = a, det * ia
     out = []
     for g in range(G):
-        d = ds[8 * g]
+        d = diag[8 * g]
         for i in range(1, 8):
-            d = jnp.where(sub8 == i, ds[8 * g + i], d)
-        s = lax.rsqrt(d)
-        out.append(jnp.concatenate([x * s for x in r[g]], axis=1))
+            d = jnp.where(sub == i, diag[8 * g + i], d)
+        scale = lax.rsqrt(d)
+        h0, w = o // 128, o % 128
+        done = 8 * g // SUB * SUB + SUB
+        if done < LEAF:
+            r[g][h0] = jnp.where((lane >= w + done) & (lane < w + LEAF), 0.0, r[g][h0])
+        out.append(jnp.concatenate([x * scale for x in r[g]], axis=1))
     return jnp.concatenate(out, axis=0)
 
 
@@ -115,7 +125,11 @@
             a_ref[pl.ds(o + LEAF, left), :] = old - upd
 
 
-def dot6(ls, rs):
+def dot_t(a, b):
+    return lax.dot_general(a, b, (((1,), (1,)), ((), ())), preferred_element_type=f32)
+
+
+def dot6(ls, rs, dot=dot):
     lh, lm, ll = ls
     rh, rm, rl = rs
     return (dot(ll, rh) + dot(lh, rl) + dot(lm, rm)) + (dot(lm, rh) + dot(lh, rm)) + dot(lh, rh)
@@ -151,17 +165,18 @@
         kpc = kpc + jnp.where(cid == ids, 0.1, 0.0)
         factor(a_ref)
         w = a_ref[...]
-        pc = dot6(split3(w), split3(kpc))
+        ws = split3(w)
+        for q, x in enumerate(ws):
+            wt_ref[q] = x
+        pc = dot6(ws, split3(kpc))
         for q, x in enumerate(split3(pc)):
             pc_ref[q] = x
-        for q, x in enumerate(split3(w.T)):
-            wt_ref[q] = x
 
     fr = fr_ref[pl.ds(pl.multiple_of(t * tile, tile), tile), :]
     krp = jnp.exp(dot(fr, fp_ref[...]))
     rid = row0 + lax.broadcasted_iota(jnp.int32, (tile, PIV), 0)
     krp = krp + jnp.where(rid == piv, 0.1, 0.0)
-    panel = dot6(split3(krp), (wt_ref[0], wt_ref[1], wt_ref[2]))
+    panel = dot6(split3(krp), (wt_ref[0], wt_ref[1], wt_ref[2]), dot_t)
     panel_ref[...] = panel
     krc = jnp.exp(dot(fr, fc_ref[...]))
     i = lax.broadcasted_iota(jnp.int32, (tile, n_cols), 0)
@@ -170,7 +185,7 @@
     schur_ref[...] = krc - dot6(split3(panel), (pc_ref[0], pc_ref[1], pc_ref[2]))
 
 
-def compute(pid, pt, fr, fc, tile=256):
+def compute(pid, pt, fr, fc, tile=512):
     n_rows, n_cols = fr.shape[0], fc.shape[1]
     vmem = pl.BlockSpec(memory_space=pltpu.VMEM)
     return pl.pallas_call(

time: 49.2 us -> 46.9 us (0.953)
  Pallas kernels: 48.4 us -> 46.1 us
    pallas_call x1, Pallas kernels: 15.2 us -> 12.9 us  [compute(): pl.pallas_call(functools.partial(kernel_b, tile=tile), grid=(n_rows // ti...]
where the time goes in v3:
time: 46.9 us; the launch traced here: 46.8 us
  Pallas kernels  46.1 us (98%)
  between operations  0.64 us (1%)
    pallas_call x1, Pallas kernels, gather(): pl.pallas_call(functools.partial(gather_kernel, nz, ny), out_shape=(pltpu...  33.3 us
    pallas_call x1, Pallas kernels, compute(): pl.pallas_call(functools.partial(kernel_b, tile=tile), grid=(n_rows // ti...  12.9 us

profile of v3, /device:TPU:1, one launch (start us, length us, event | category | flops | bytes accessed | tf_op | source)
XLA Modules:
  0.0 46.8 jit_solution(7605661516783147740)
XLA Ops:
  0.6 33.3 %shard_map.50 = (s32[1,256]{1,0:T(1,128)S(1)}, f32[2,16,128]{2,1,0:T(8,128)S(1)}, bf16[1024,128]{1,0:T(8,128)(2,1)S(1)}, bf16[128,512]{1,0:T(8,128)(2,1)S(1)}) custom-call(f32[16,32]{1,0:T(8,128)} %pts_hbm.1, s32[1,128]{1,0:T(1,128)} %bitcast.2, s32[1,128]{1,0:T(1,128)} %bitcast.3), custom_call_target="tpu_custom_call" | custom-call | tf_op jit(solution)/shard_map/pallas_call | solution.py:413
  33.9 12.9 %shard_map.51 = (f32[1024,256]{1,0:T(8,128)}, f32[1024,512]{1,0:T(8,128)}) custom-call(s32[1,256]{1,0:T(1,128)S(1)} %get-tuple-element.6.pid_ref, f32[2,16,128]{2,1,0:T(8,128)S(1)} %get-tuple-element.7.pt_ref, bf16[1024,128]{1,0:T(8,128)(2,1)S(1)} %get-tuple-element.8.fr_ref, bf16[128,512]{1,0:T(8,128)(2,1)S(1)} %get-tuple-element.9.fc_ref), custom_call_target="tpu_custom_call" | custom-call | tf_op jit(solution)/shard_map/pallas_call | solution.py:191

commit v4 on v3

--- a/solution.py
+++ b/solution.py
@@ -141,7 +141,7 @@
     return (dot(lm, rh) + dot(lh, rm)) + dot(lh, rh)
 
 
-def kernel_b(pid_ref, pt_ref, fr_ref, fc_ref, panel_ref, schur_ref,
+def kernel_b(pid_ref, pt_ref, fr_ref, fc_ref, krc_ref, panel_ref, schur_ref,
              a_ref, fp_ref, wt_ref, pc_ref, *, tile):
     t = pl.program_id(0)
     n_cols = fc_ref.shape[1]
@@ -178,14 +178,11 @@
     krp = krp + jnp.where(rid == piv, 0.1, 0.0)
     panel = dot6(split3(krp), (wt_ref[0], wt_ref[1], wt_ref[2]), dot_t)
     panel_ref[...] = panel
-    krc = jnp.exp(dot(fr, fc_ref[...]))
-    i = lax.broadcasted_iota(jnp.int32, (tile, n_cols), 0)
-    j = lax.broadcasted_iota(jnp.int32, (tile, n_cols), 1)
-    krc = krc + jnp.where(i - j == col0 - row0, 0.1, 0.0)
+    krc = krc_ref[pl.ds(pl.multiple_of(t * tile, tile), tile), :]
     schur_ref[...] = krc - dot6(split3(panel), (pc_ref[0], pc_ref[1], pc_ref[2]))
 
 
-def compute(pid, pt, fr, fc, tile=512):
+def compute(pid, pt, fr, fc, krc, tile=512):
     n_rows, n_cols = fr.shape[0], fc.shape[1]
     vmem = pl.BlockSpec(memory_space=pltpu.VMEM)
     return pl.pallas_call(
@@ -195,7 +192,7 @@
             jax.ShapeDtypeStruct((n_rows, PIV), f32),
             jax.ShapeDtypeStruct((n_rows, n_cols), f32),
         ),
-        in_specs=[vmem] * 4,
+        in_specs=[vmem] * 5,
         out_specs=(
             pl.BlockSpec((tile, PIV), lambda t: (t, 0)),
             pl.BlockSpec((tile, n_cols), lambda t: (t, 0)),
@@ -207,7 +204,7 @@
             pltpu.VMEM((3, PIV, n_cols), bf16),
         ],
         compiler_params=pltpu.CompilerParams(vmem_limit_bytes=32 << 20),
-    )(pid, pt, fr, fc)
+    )(pid, pt, fr, fc, krc)
 
 
 MESH = pl.DeviceIdType.MESH
@@ -237,7 +234,7 @@
             out_ref[4 * g:4 * g + 4, 128 * t:128 * t + 128] = acc[4 * t:4 * t + 4]
 
 
-def gather_kernel(nz, ny, pts_hbm, pf_hbm, ps_hbm, pid_out, piv_out, fr_out, fc_out,
+def gather_kernel(nz, ny, pts_hbm, pf_hbm, ps_hbm, pid_out, piv_out, fr_out, fc_out, krc_out,
                   pts_ref, in_sem, own, contrib, c_buf, x_src, x_buf, y_src, y_buf, z_src, z_buf,
                   row_buf, col_buf, rt_ref, ct_ref,
                   c_send, c_recv, x_send, x_recv, y_send, y_recv, z_send, z_recv, ag_send, ag_recv,
@@ -280,9 +277,6 @@
     def signal(dev):
         pl.semaphore_signal(barrier, inc=1, device_id=dev, device_id_type=MESH)
 
-    signal(other)
-    loop(1, nz, lambda d: signal(z_dev(d)))
-    loop(1, n_col, lambda d: signal(row_dev(d)))
 
     def greet_source(i):
         @pl.when(jnp.logical_or(source != row, first + i != col))
@@ -290,6 +284,9 @@
             signal((source, first + i))
 
     loop(0, per, greet_source)
+    loop(1, nz, lambda d: signal(z_dev(d)))
+    loop(1, n_col, lambda d: signal(row_dev(d)))
+    signal(other)
 
     for a in arrivals:
         a.wait()
@@ -379,6 +376,18 @@
     unpack(col_buf, ct_ref)
     fr_out[...] = features(rt_ref[...], True).T
     fc_out[...] = features(ct_ref[...], False)
+    n_cols = fc_out.shape[1]
+    off = col * n_cols - row * fr_out.shape[0]
+    step = 256
+
+    def block(b):
+        at = pl.ds(pl.multiple_of(b * step, step), step)
+        i = b * step + lax.broadcasted_iota(jnp.int32, (step, n_cols), 0)
+        j = off + lax.broadcasted_iota(jnp.int32, (step, n_cols), 1)
+        k = jnp.exp(dot(fr_out[at, :], fc_out[...]))
+        krc_out[at, :] = k + jnp.where(i == j, 0.1, 0.0)
+
+    loop(0, fr_out.shape[0] // step, block)
 
     for d in range(1, nz):
         z_copy(d).wait_recv()
@@ -417,9 +426,10 @@
             pltpu.VMEM((2, DIM, BLOCK), f32),
             pltpu.VMEM((n * n_col, 128), bf16),
             pltpu.VMEM((128, n * n_row), bf16),
+            pltpu.VMEM((n * n_col, n * n_row), f32),
         ),
         in_specs=[pl.BlockSpec(memory_space=pltpu.HBM)] * 3,
-        out_specs=(vmem,) * 4,
+        out_specs=(vmem,) * 5,
         scratch_shapes=[
             pltpu.VMEM((DIM, n), f32),
             dma((3,)),

time: 46.9 us -> 46 us (0.981)
  Pallas kernels: 46.1 us -> 45.2 us
    pallas_call x1, Pallas kernels: 33.3 us -> 32.7 us  [gather(): pl.pallas_call(functools.partial(gather_kernel, nz, ny), out_shape=(pltpu...]
where the time goes in v4:
time: 46 us; the launch traced here: 45.9 us
  Pallas kernels  45.2 us (98%)
  between operations  0.64 us (1%)
    pallas_call x1, Pallas kernels, gather(): pl.pallas_call(functools.partial(gather_kernel, nz, ny), out_shape=(pltpu...  32.7 us
    pallas_call x1, Pallas kernels, compute(): pl.pallas_call(functools.partial(kernel_b, tile=tile), grid=(n_rows // ti...  12.6 us

profile of v4, /device:TPU:1, one launch (start us, length us, event | category | flops | bytes accessed | tf_op | source)
XLA Modules:
  0.0 45.9 jit_solution(12551478896470561404)
XLA Ops:
  0.6 32.7 %shard_map.50 = (s32[1,256]{1,0:T(1,128)S(1)}, f32[2,16,128]{2,1,0:T(8,128)S(1)}, bf16[1024,128]{1,0:T(8,128)(2,1)S(1)}, bf16[128,512]{1,0:T(8,128)(2,1)S(1)}, f32[1024,512]{1,0:T(8,128)S(1)}) custom-call(f32[16,32]{1,0:T(8,128)} %pts_hbm.1, s32[1,128]{1,0:T(1,128)} %bitcast.2, s32[1,128]{1,0:T(1,128)} %bitcast.3), custom_call_target="tpu_custom_call" | custom-call | tf_op jit(solution)/shard_map/pallas_call | solution.py:422
  33.3 12.6 %shard_map.51 = (f32[1024,256]{1,0:T(8,128)}, f32[1024,512]{1,0:T(8,128)}) custom-call(s32[1,256]{1,0:T(1,128)S(1)} %get-tuple-element.7.pid_ref, f32[2,16,128]{2,1,0:T(8,128)S(1)} %get-tuple-element.8.pt_ref, bf16[1024,128]{1,0:T(8,128)(2,1)S(1)} %get-tuple-element.9.fr_ref, bf16[128,512]{1,0:T(8,128)(2,1)S(1)} %get-tuple-element.10.fc_ref, ...), custom_call_target="tpu_custom_call" | custom-call | tf_op jit(solution)/shard_map/pallas_call | solution.py:188

commit v5 on v4

--- a/solution.py
+++ b/solution.py
@@ -141,67 +141,80 @@
     return (dot(lm, rh) + dot(lh, rm)) + dot(lh, rh)
 
 
-def kernel_b(pid_ref, pt_ref, fr_ref, fc_ref, krc_ref, panel_ref, schur_ref,
-             a_ref, fp_ref, wt_ref, pc_ref, *, tile):
-    t = pl.program_id(0)
-    n_cols = fc_ref.shape[1]
-    row0 = lax.axis_index("row") * fr_ref.shape[0] + t * tile
+def kernel_b(pid_ref, pt_ref, fr_ref, fc_ref, krc_ref, panel_hbm, schur_hbm,
+             a_ref, kr_ref, kc_ref, pc_ref, panel_ref, schur_ref, sems, *, tile):
+    n_rows, n_cols = krc_ref.shape
+    row0 = lax.axis_index("row") * n_rows
     col0 = lax.axis_index("col") * n_cols
     piv = pid_ref[...]
-
-    @pl.when(t == 0)
-    def _():
-        pt = jnp.concatenate([pt_ref[0], pt_ref[1]], axis=1)
-        fp = features(pt, False)
-        fp_ref[...] = fp
-        fpl = features(pt, True).T
-        kpp = jnp.exp(dot(fpl, fp))
-        i = lax.broadcasted_iota(jnp.int32, (PIV, PIV), 0)
-        j = lax.broadcasted_iota(jnp.int32, (PIV, PIV), 1)
-        a_ref[...] = jnp.where(i == j, kpp + 0.1, kpp)
-        kpc = jnp.exp(dot(fpl, fc_ref[...]))
-        ids = jnp.broadcast_to(piv.astype(f32), (8, PIV)).T[:, 0:1].astype(jnp.int32)
-        cid = col0 + lax.broadcasted_iota(jnp.int32, (PIV, n_cols), 1)
-        kpc = kpc + jnp.where(cid == ids, 0.1, 0.0)
-        factor(a_ref)
-        w = a_ref[...]
-        ws = split3(w)
-        for q, x in enumerate(ws):
-            wt_ref[q] = x
-        pc = dot6(ws, split3(kpc))
-        for q, x in enumerate(split3(pc)):
-            pc_ref[q] = x
-
-    fr = fr_ref[pl.ds(pl.multiple_of(t * tile, tile), tile), :]
-    krp = jnp.exp(dot(fr, fp_ref[...]))
-    rid = row0 + lax.broadcasted_iota(jnp.int32, (tile, PIV), 0)
-    krp = krp + jnp.where(rid == piv, 0.1, 0.0)
-    panel = dot6(split3(krp), (wt_ref[0], wt_ref[1], wt_ref[2]), dot_t)
-    panel_ref[...] = panel
-    krc = krc_ref[pl.ds(pl.multiple_of(t * tile, tile), tile), :]
-    schur_ref[...] = krc - dot6(split3(panel), (pc_ref[0], pc_ref[1], pc_ref[2]))
-
-
-def compute(pid, pt, fr, fc, krc, tile=512):
-    n_rows, n_cols = fr.shape[0], fc.shape[1]
+    pt = jnp.concatenate([pt_ref[0], pt_ref[1]], axis=1)
+    fp = features(pt, False)
+    fpl = features(pt, True).T
+    kpp = jnp.exp(dot(fpl, fp))
+    i = lax.broadcasted_iota(jnp.int32, (PIV, PIV), 0)
+    j = lax.broadcasted_iota(jnp.int32, (PIV, PIV), 1)
+    a_ref[...] = jnp.where(i == j, kpp + 0.1, kpp)
+    kpc = jnp.exp(dot(fpl, fc_ref[...]))
+    ids = jnp.broadcast_to(piv.astype(f32), (8, PIV)).T[:, 0:1].astype(jnp.int32)
+    cid = col0 + lax.broadcasted_iota(jnp.int32, (PIV, n_cols), 1)
+    kpc = kpc + jnp.where(cid == ids, 0.1, 0.0)
+    for q, x in enumerate(split3(kpc)):
+        kc_ref[q] = x
+    for t in range(0, n_rows, 256):
+        krp = jnp.exp(dot(fr_ref[t:t + 256, :], fp))
+        rid = row0 + t + lax.broadcasted_iota(jnp.int32, (256, PIV), 0)
+        krp = krp + jnp.where(rid == piv, 0.1, 0.0)
+        for q, x in enumerate(split3(krp)):
+            kr_ref[q, t:t + 256, :] = x
+
+    factor(a_ref)
+    ws = split3(a_ref[...])
+    pc = dot6(ws, (kc_ref[0], kc_ref[1], kc_ref[2]))
+    for q, x in enumerate(split3(pc)):
+        pc_ref[q] = x
+
+    copies = []
+
+    def send(src, dst):
+        copy = pltpu.make_async_copy(src, dst, sems.at[len(copies)])
+        copy.start()
+        copies.append(copy)
+
+    half = n_cols // 2
+    for t in range(0, n_rows, tile):
+        rows = pl.ds(t, tile)
+        panel = dot6(tuple(kr_ref[q, t:t + tile, :] for q in range(3)), ws, dot_t)
+        panel_ref[rows, :] = panel
+        send(panel_ref.at[rows, :], panel_hbm.at[rows, :])
+        ps = split3(panel)
+        for c in range(0, n_cols, half):
+            cols = pl.ds(c, half)
+            schur_ref[rows, cols] = krc_ref[rows, cols] - dot6(ps, tuple(pc_ref[q, :, c:c + half] for q in range(3)))
+            send(schur_ref.at[rows, cols], schur_hbm.at[rows, cols])
+    for copy in copies:
+        copy.wait()
+
+
+def compute(pid, pt, fr, fc, krc, tile=1024):
+    n_rows, n_cols = krc.shape
     vmem = pl.BlockSpec(memory_space=pltpu.VMEM)
+    hbm = pl.BlockSpec(memory_space=pltpu.HBM)
     return pl.pallas_call(
         functools.partial(kernel_b, tile=tile),
-        grid=(n_rows // tile,),
         out_shape=(
             jax.ShapeDtypeStruct((n_rows, PIV), f32),
             jax.ShapeDtypeStruct((n_rows, n_cols), f32),
         ),
         in_specs=[vmem] * 5,
-        out_specs=(
-            pl.BlockSpec((tile, PIV), lambda t: (t, 0)),
-            pl.BlockSpec((tile, n_cols), lambda t: (t, 0)),
-        ),
+        out_specs=(hbm, hbm),
         scratch_shapes=[
             pltpu.VMEM((PIV, PIV), f32),
-            pltpu.VMEM((128, PIV), bf16),
-            pltpu.VMEM((3, PIV, PIV), bf16),
+            pltpu.VMEM((3, n_rows, PIV), bf16),
             pltpu.VMEM((3, PIV, n_cols), bf16),
+            pltpu.VMEM((3, PIV, n_cols), bf16),
+            pltpu.VMEM((n_rows, PIV), f32),
+            pltpu.VMEM((n_rows, n_cols), f32),
+            pltpu.SemaphoreType.DMA((3 * n_rows // tile,)),
         ],
         compiler_params=pltpu.CompilerParams(vmem_limit_bytes=32 << 20),
     )(pid, pt, fr, fc, krc)

time: 46 us -> 44.1 us (0.959)
  Pallas kernels: 45.2 us -> 43.4 us
    pallas_call x1, Pallas kernels: 12.6 us -> 10.7 us  [compute(): pl.pallas_call(functools.partial(kernel_b, tile=tile), out_shape=(jax.Sha...]
where the time goes in v5:
time: 44.1 us; the launch traced here: 44 us
  Pallas kernels  43.4 us (98%)
  between operations  0.64 us (1%)
    pallas_call x1, Pallas kernels, gather(): pl.pallas_call(functools.partial(gather_kernel, nz, ny), out_shape=(pltpu...  32.7 us
    pallas_call x1, Pallas kernels, compute(): pl.pallas_call(functools.partial(kernel_b, tile=tile), out_shape=(jax.Sha...  10.7 us

profile of v5, /device:TPU:1, one launch (start us, length us, event | category | flops | bytes accessed | tf_op | source)
XLA Modules:
  0.0 44.0 jit_solution(8714120712490288063)
XLA Ops:
  0.6 32.7 %shard_map.50 = (s32[1,256]{1,0:T(1,128)S(1)}, f32[2,16,128]{2,1,0:T(8,128)S(1)}, bf16[1024,128]{1,0:T(8,128)(2,1)S(1)}, bf16[128,512]{1,0:T(8,128)(2,1)S(1)}, f32[1024,512]{1,0:T(8,128)S(1)}) custom-call(f32[16,32]{1,0:T(8,128)} %pts_hbm.1, s32[1,128]{1,0:T(1,128)} %bitcast.2, s32[1,128]{1,0:T(1,128)} %bitcast.3), custom_call_target="tpu_custom_call" | custom-call | tf_op jit(solution)/shard_map/pallas_call | solution.py:435
  33.3 10.7 %shard_map.51 = (f32[1024,256]{1,0:T(8,128)}, f32[1024,512]{1,0:T(8,128)}) custom-call(s32[1,256]{1,0:T(1,128)S(1)} %get-tuple-element.7.pid_ref, f32[2,16,128]{2,1,0:T(8,128)S(1)} %get-tuple-element.8.pt_ref, bf16[1024,128]{1,0:T(8,128)(2,1)S(1)} %get-tuple-element.9.fr_ref, bf16[128,512]{1,0:T(8,128)(2,1)S(1)} %get-tuple-element.10.fc_ref, ...), custom_call_target="tpu_custom_call" | custom-call | tf_op jit(solution)/shard_map/pallas_call | solution.py:202
